TPU v7x, 32 devices: a whole 2x2x4 slice. The times are simulated.
32 devices in a mesh: gx: 4 (over z), gy: 2 (over y), gz: 4 (over x, core).
Axes of the slice: x: 2, y: 2, z: 4, core: 2. Of those that a mesh axis runs over, the one named last changes fastest.
Arguments:
- cell_volume: float32 [64, 32, 512], P('gx', 'gy', 'gz'), may hold values from 0.5 to 2
- exponent: int32 [64, 32, 512], P('gx', 'gy', 'gz'), may hold values from 0 to 7
- owner_row: int32 [8192], P(('gx', 'gy', 'gz')), may hold values from 0 to 8191, as said below
Outputs:
- stencil_out: float32 [27, 8192, 128], P(None, ('gx', 'gy', 'gz'))
- lumped_out: float32 [8192, 128], P(('gx', 'gy', 'gz'))
Inputs may be any that keep to these rules, and one draw needn't show every extreme that they name: owner_row is a permutation of the row blocks; the row blocks of each device's share of owner_row go to each owner (owner_row // 256) exactly 8 times.
All inputs are finite; a program needn't handle non-finite values.
Results may differ from a plain program's by a relative error of at most 0.00007.
Values sent between devices are 32-bit elements; how exact they have to be, the bound alone decides.
A program may use at most 64 MiB of HBM per device.

v0:
```python
import jax
import jax.numpy as jnp
import numpy as np
from jax import lax
from jax.sharding import PartitionSpec as P

log_step = 0.3


def from_behind(block, axis, distance):
    devices = range(lax.axis_size(axis))
    route = [((i - distance) % len(devices), i) for i in devices]
    return lax.ppermute(block, axis, route)


def weight_table():
    table = np.zeros((27, 8), np.float32)
    for index_o in range(27):
        offsets = (index_o // 9 - 1, index_o // 3 % 3 - 1, index_o % 3 - 1)
        for index_a in range(8):
            corner = (index_a // 4, index_a // 2 % 2, index_a % 2)
            inside = all((0 <= corner[slot_d] + offsets[slot_d] <= 1 for slot_d in range(3)))
            factor = 1.0
            for slot_d in range(3):
                factor = factor * (2.0 if offsets[slot_d] == 0 else 1.0)
            table[index_o, index_a] = factor / 64.0 if inside else 0.0
    return table


def rim_section(current, along, stack_at, sender):
    length = current.shape[along]
    interior = lax.slice_in_dim(current, 0, length - 1, axis=along)
    top_layer = lax.slice_in_dim(current, length - 1, length, axis=along)
    received = sender(top_layer)
    behind = jnp.concatenate([received, interior], axis=along)
    return jnp.stack([current, behind], axis=stack_at)


def shards(cell_volume, exponent, owner_row):
    weight = cell_volume * jnp.exp(-log_step * exponent.astype(jnp.float32))
    span_x, span_y, span_z = weight.shape
    line_count = span_x * span_y
    devices_all = lax.axis_size(("gx", "gy", "gz"))

    def send_x(rim_layer):
        return from_behind(rim_layer, "gx", 1)

    def send_y(rim_layer):
        return from_behind(rim_layer, "gy", 1)

    owner_dev = owner_row // line_count
    by_owner = jnp.argsort(owner_dev, stable=True)
    slot_ids = (owner_row % line_count)[by_owner].reshape(1, devices_all, -1)
    table = jnp.asarray(weight_table())
    sectioned_x = rim_section(weight, 0, 0, send_x)
    sectioned_xy = rim_section(sectioned_x, 2, 1, send_y)
    lines = sectioned_xy.reshape(4, line_count, span_z)
    rim_values = from_behind(sectioned_xy[..., span_z - 1 :], "gz", 1).reshape(4, line_count)
    packed = lines[:, by_owner].reshape(4, devices_all, -1, span_z)
    rim_packed = rim_values[:, by_owner].reshape(4, devices_all, -1)
    got_lines, got_rims, got_slots = (
        lax.all_to_all(packed, ("gx", "gy", "gz"), split_axis=1, concat_axis=1, tiled=True),
        lax.all_to_all(rim_packed, ("gx", "gy", "gz"), split_axis=1, concat_axis=1, tiled=True),
        lax.all_to_all(slot_ids, ("gx", "gy", "gz"), split_axis=1, concat_axis=1, tiled=True),
    )
    placing = jnp.argsort(got_slots.reshape(-1))
    current = got_lines.reshape(4, line_count, span_z)[:, placing]
    before = got_rims.reshape(4, line_count)[:, placing]
    behind = jnp.concatenate([before[..., None], current[..., : span_z - 1]], axis=2)
    corners = jnp.stack([current, behind], axis=1).reshape(8, line_count, span_z)
    stencil_rows = jnp.einsum("oa,alz->olz", table, corners, precision=lax.Precision.HIGHEST)
    lumped_rows = 1.0 / jnp.sum(stencil_rows, axis=0)
    return (stencil_rows, lumped_rows)


def solution(mesh):
    return jax.shard_map(
        shards,
        mesh=mesh,
        in_specs=(P("gx", "gy", "gz"), P("gx", "gy", "gz"), P(("gx", "gy", "gz"))),
        out_specs=(P(None, ("gx", "gy", "gz"), None), P(("gx", "gy", "gz"), None)),
        check_vma=False,
    )
```

profile of v0, /device:TPU:0, one launch (start us, length us, event | category | flops | bytes accessed | tf_op | source)
XLA Modules:
  0.0 66.7 jit_solution(13630262406832950411)
XLA Ops:
  0.6 1.0 %exponential_multiply_fusion = f32[16,16,128]{2,1,0:T(8,128)S(1)} fusion(f32[16,16,128]{2,1,0:T(8,128)} %param.4, s32[16,16,128]{2,1,0:T(8,128)} %param.5), kind=kLoop, calls=%fused_computation.20 | loop fusion | flops 98304 | bytes 393216 | tf_op jit(solution)/shard_map/mul | solution.py:40
  1.6 3.1 %collective-permute-start = (f32[1,16,128]{2,1,0:T(8,128)S(1)}, f32[1,16,128]{2,1,0:T(8,128)S(1)}, u32[]{:S(2)}, u32[]{:S(2)}) collective-permute-start(f32[1,16,128]{2,1,0:T(8,128)S(1)} %slice.34), channel_id=1, source_target_pairs={{24,0},{0,8},{8,16},{16,24},{25,1},{1,9},{9,17},{17,25},{26,2},{2,... | collective-permute-start | bytes 24584 | tf_op jit(solution)/shard_map/ppermute | solution.py:13
  4.7 0.7 %and_select_fusion = (s32[256]{0:T(256)S(1)}, s32[256]{0:T(256)S(1)}) fusion(s32[256]{0:T(256)} %param.6), kind=kLoop, calls=%fused_computation.27 | loop fusion | flops 4864 | bytes 3072 | tf_op jit(solution)/shard_map/jit(remainder)/select_n | solution.py:53
  5.4 3.2 %sort.34 = (s32[256]{0:T(256)}, s32[256]{0:T(256)S(1)}) sort(s32[256]{0:T(256)S(1)} %get-tuple-element.15, s32[256]{0:T(256)S(1)} %iota.8), dimensions={0}, to_apply=%region_0.1 | sort | flops 2048 | bytes 4096 | tf_op jit(solution)/shard_map/jit(argsort)/sort | solution.py:52
  8.7 1.6 %collective-permute-start.1 = (f32[2,16,1,128]{3,2,1,0:T(1,128)S(1)}, f32[2,16,1,128]{3,2,1,0:T(1,128)S(1)}, u32[]{:S(2)}, u32[]{:S(2)}) collective-permute-start(f32[2,16,1,128]{3,2,1,0:T(1,128)S(1)} %fusion.3), channel_id=1, source_target_pairs={{4,0},{0,4},{5,1},{1,5},{6,2},{2,6},{7,3},{3,7},{12,8},{8,12},{13,... | collective-permute-start | bytes 49160 | tf_op jit(solution)/shard_map/ppermute | solution.py:13
  10.3 2.2 %collective-permute-done.1 = f32[2,16,1,128]{3,2,1,0:T(1,128)S(1)} collective-permute-done((f32[2,16,1,128]{3,2,1,0:T(1,128)S(1)}, f32[2,16,1,128]{3,2,1,0:T(1,128)S(1)}, u32[]{:S(2)}, u32[]{:S(2)}) %collective-permute-start.1) | collective-permute-done | bytes 16416 | tf_op jit(solution)/shard_map/ppermute | solution.py:13
  12.8 1.9 %gather_fusion.1 = s32[256]{0:T(256)S(1)} fusion(s32[256]{0:T(256)S(1)} %get-tuple-element.14, s32[1024]{0:T(1024)S(1)} %pad_clamp_fusion.1), kind=kCustom, calls=%fused_computation.1 | custom fusion | bytes 3072 | tf_op jit(solution)/shard_map/gather | solution.py:53
  14.8 0.7 %reshape.34 = s32[1,32,8]{2,1,0:T(8,128)} reshape(s32[256]{0:T(256)S(1)} %gather_fusion.1) | data formatting | bytes 2048 | tf_op jit(solution)/shard_map/reshape | solution.py:53
  15.5 5.1 %all-to-all-start.1 = ((s32[1,32,8]{2,0,1:T(1,128)}), s32[1,32,8]{2,0,1:T(1,128)S(1)}, u32[]{:S(2)}, u32[]{:S(2)}) async-start(s32[1,32,8]{2,0,1:T(1,128)} %bitcast.10), calls=%async_computation.1 | async-start | bytes 32768 | tf_op jit(solution)/shard_map/all_to_all | solution.py:64
  20.6 0.8 %collective-permute-done.2 = f32[2,2,16,16,1]{4,3,2,1,0:T(8,128)S(1)} collective-permute-done((f32[2,2,16,16,1]{4,3,2,1,0:T(8,128)S(1)}, f32[2,2,16,16,1]{4,3,2,1,0:T(8,128)S(1)}, u32[]{:S(2)}, u32[]{:S(2)}) %collective-permute-start.2) | collective-permute-done | bytes 4128 | tf_op jit(solution)/shard_map/ppermute | solution.py:13
  21.8 0.7 %gather_fusion.3 = f32[256,4]{1,0:T(8,128)S(1)} fusion(f32[4,256]{0,1:T(8,128)S(1)} %copy.25, s32[1024]{0:T(1024)S(1)} %pad_clamp_fusion.1), kind=kCustom, calls=%fused_computation.3 | custom fusion | bytes 9216 | tf_op jit(solution)/shard_map/gather | solution.py:60
  22.6 0.9 %copy.26 = f32[4,32,8]{2,0,1:T(4,128)} copy(f32[4,32,8]{0,2,1:T(8,128)S(1)} %bitcast.45) | data formatting | bytes 8192 | tf_op jit(solution)/shard_map/reshape | solution.py:60
  23.5 4.2 %all-to-all-done.1 = s32[1,32,8]{2,0,1:T(1,128)S(1)} async-done(((s32[1,32,8]{2,0,1:T(1,128)}), s32[1,32,8]{2,0,1:T(1,128)S(1)}, u32[]{:S(2)}, u32[]{:S(2)}) %all-to-all-start.1) | async-done | bytes 1056 | tf_op jit(solution)/shard_map/all_to_all | solution.py:64
  27.7 2.6 %all-to-all-start.2 = ((f32[4,32,8]{2,0,1:T(4,128)}), f32[4,32,8]{2,0,1:T(4,128)S(1)}, u32[]{:S(2)}, u32[]{:S(2)}) async-start(f32[4,32,8]{2,0,1:T(4,128)} %copy.26), calls=%async_computation.2 | async-start | bytes 131072 | tf_op jit(solution)/shard_map/all_to_all | solution.py:63
  30.3 0.3 copy.23
  30.7 1.8 %gather_fusion = f32[256,4,128]{2,1,0:T(4,128)} fusion(f32[4,256,128]{2,0,1:T(4,128)S(1)} %copy.23, s32[1024]{0:T(1024)S(1)} %pad_clamp_fusion.1), kind=kCustom, calls=%fused_computation | custom fusion | bytes 1049600 | tf_op jit(solution)/shard_map/gather | solution.py:59
  32.4 5.3 %all-to-all-done.2 = f32[4,32,8]{2,0,1:T(4,128)S(1)} async-done(((f32[4,32,8]{2,0,1:T(4,128)}), f32[4,32,8]{2,0,1:T(4,128)S(1)}, u32[]{:S(2)}, u32[]{:S(2)}) %all-to-all-start.2) | async-done | bytes 4128 | tf_op jit(solution)/shard_map/all_to_all | solution.py:63
  37.7 2.9 %all-to-all-start = ((f32[4,32,8,128]{3,0,2,1:T(4,128)}), f32[4,32,8,128]{3,0,2,1:T(4,128)S(1)}, u32[]{:S(2)}, u32[]{:S(2)}) async-start(f32[4,32,8,128]{3,0,2,1:T(4,128)} %bitcast.8), calls=%async_computation | async-start | bytes 1048576 | tf_op jit(solution)/shard_map/all_to_all | solution.py:62
  40.6 0.5 broadcast.55
  41.1 0.7 %reduce.4 = s32[32,8]{1,0:T(8,128)S(1)} reduce(s32[1,32,8]{2,0,1:T(1,128)S(1)} %all-to-all-done.1, s32[]{:T(128)} %broadcast.55), dimensions={0}, to_apply=%all_to_all.10.reduce_sub_computation.3 | reduce | bytes 2052 | tf_op jit(solution)/shard_map/all_to_all | solution.py:64
  41.9 3.2 %sort.35 = (s32[256]{0:T(256)}, s32[256]{0:T(256)S(1)}) sort(s32[256]{0:T(256)S(1)} %reshape.35, s32[256]{0:T(256)S(1)} %iota.9), dimensions={0}, to_apply=%region_1.2 | sort | flops 2048 | bytes 4096 | tf_op jit(solution)/shard_map/jit(argsort)/sort | solution.py:66
  45.1 0.3 copy.27
  45.3 0.7 %gather_fusion.4 = f32[256,4]{1,0:T(8,128)S(1)} fusion(f32[4,256]{0,1:T(8,128)S(1)} %bitcast.43, s32[1024]{0:T(1024)S(1)} %pad_clamp_fusion), kind=kCustom, calls=%fused_computation.4 | custom fusion | bytes 9216 | tf_op jit(solution)/shard_map/gather | solution.py:68
  46.1 1.7 %copy.29 = f32[4,256,1]{2,0,1:T(4,128)S(1)} copy(f32[4,256,1]{0,1,2:T(8,128)S(1)} %bitcast.44) | data formatting | bytes 8192 | tf_op jit(solution)/shard_map/broadcast_in_dim | solution.py:69
  47.7 8.3 %all-to-all-done = f32[4,32,8,128]{3,0,2,1:T(4,128)S(1)} async-done(((f32[4,32,8,128]{3,0,2,1:T(4,128)}), f32[4,32,8,128]{3,0,2,1:T(4,128)S(1)}, u32[]{:S(2)}, u32[]{:S(2)}) %all-to-all-start) | async-done | bytes 524320 | tf_op jit(solution)/shard_map/all_to_all | solution.py:62
  56.0 1.0 %gather_fusion.2 = f32[256,4,128]{2,1,0:T(4,128)S(1)} fusion(f32[4,256,128]{2,0,1:T(4,128)S(1)} %bitcast.41, s32[1024]{0:T(1024)S(1)} %pad_clamp_fusion), kind=kCustom, calls=%fused_computation.2 | custom fusion | bytes 1049600 | tf_op jit(solution)/shard_map/gather | solution.py:67
  57.0 0.3 maximum_bitcast_fusion
  57.4 0.2 pad_maximum_fusion
  57.6 0.8 %copy.30 = f32[4,2,256,128]{3,1,0,2:T(2,128)S(1)} copy(f32[4,2,256,128]{3,0,2,1:T(4,128)S(1)} %pad_maximum_fusion) | data formatting | bytes 2097152 | tf_op jit(solution)/shard_map/stack | solution.py:70
  58.4 3.7 %fusion.4 = (f32[256,128]{1,0:T(8,128)S(1)}, f32[27,256,128]{2,0,1:T(8,128)S(1)}) fusion(f32[27,8,1]{0,1,2:T(8,128)S(1)} %copy-done, f32[8,256,128]{2,0,1:T(8,128)S(1)} %bitcast.37), kind=kOutput, calls=%fused_computation.34 | convolution fusion | flops 85786624 | bytes 4719456 | tf_op jit(solution)/shard_map/oa,alz->olz/dot_general | solution.py:71
  62.2 0.7 %broadcast_divide_fusion = f32[256,128]{1,0:T(8,128)} fusion(f32[256,128]{1,0:T(8,128)S(1)} %get-tuple-element.16), kind=kLoop, calls=%fused_computation.21 | loop fusion | flops 32768 | bytes 262144 | tf_op jit(solution)/shard_map/div | solution.py:72
  62.8 3.8 %copy.31 = f32[27,256,128]{2,1,0:T(8,128)} copy(f32[27,256,128]{2,0,1:T(8,128)S(1)} %get-tuple-element.17) | data formatting | bytes 7077888
  (23 shorter events, 1.0 us)
Async XLA Ops:
  1.6 7.0 %collective-permute-start = (f32[1,16,128]{2,1,0:T(8,128)S(1)}, f32[1,16,128]{2,1,0:T(8,128)S(1)}, u32[]{:S(2)}, u32[]{:S(2)}) collective-permute-start(f32[1,16,128]{2,1,0:T(8,128)S(1)} %slice.34), channel_id=1, source_target_pairs={{24,0},{0,8},{8,16},{16,24},{25,1},{1,9},{9,17},{17,25},{26,2},{2,... | collective-permute-start | bytes 24584 | tf_op jit(solution)/shard_map/ppermute | solution.py:13
  8.7 3.8 %collective-permute-start.1 = (f32[2,16,1,128]{3,2,1,0:T(1,128)S(1)}, f32[2,16,1,128]{3,2,1,0:T(1,128)S(1)}, u32[]{:S(2)}, u32[]{:S(2)}) collective-permute-start(f32[2,16,1,128]{3,2,1,0:T(1,128)S(1)} %fusion.3), channel_id=1, source_target_pairs={{4,0},{0,4},{5,1},{1,5},{6,2},{2,6},{7,3},{3,7},{12,8},{8,12},{13,... | collective-permute-start | bytes 49160 | tf_op jit(solution)/shard_map/ppermute | solution.py:13
  12.7 8.7 %collective-permute-start.2 = (f32[2,2,16,16,1]{4,3,2,1,0:T(8,128)S(1)}, f32[2,2,16,16,1]{4,3,2,1,0:T(8,128)S(1)}, u32[]{:S(2)}, u32[]{:S(2)}) collective-permute-start(f32[2,2,16,16,1]{4,3,2,1,0:T(8,128)S(1)} %fusion), channel_id=1, source_target_pairs={{3,0},{0,1},{1,2},{2,3},{7,4},{4,5},{5,6},{6,7},{11,8},{8,9},{9,10... | collective-permute-start | bytes 12296 | tf_op jit(solution)/shard_map/ppermute | solution.py:13
  15.5 12.2 %all-to-all-start.1 = ((s32[1,32,8]{2,0,1:T(1,128)}), s32[1,32,8]{2,0,1:T(1,128)S(1)}, u32[]{:S(2)}, u32[]{:S(2)}) async-start(s32[1,32,8]{2,0,1:T(1,128)} %bitcast.10), calls=%async_computation.1 | async-start | bytes 32768 | tf_op jit(solution)/shard_map/all_to_all | solution.py:64
  27.7 10.0 %all-to-all-start.2 = ((f32[4,32,8]{2,0,1:T(4,128)}), f32[4,32,8]{2,0,1:T(4,128)S(1)}, u32[]{:S(2)}, u32[]{:S(2)}) async-start(f32[4,32,8]{2,0,1:T(4,128)} %copy.26), calls=%async_computation.2 | async-start | bytes 131072 | tf_op jit(solution)/shard_map/all_to_all | solution.py:63
  37.7 20.8 %copy-start = (f32[27,8,1]{0,1,2:T(8,128)S(1)}, f32[27,8,1]{0,1,2:T(8,128)}, u32[]{:S(2)}) copy-start(f32[27,8,1]{0,1,2:T(8,128)} %constant.39) | copy-start | bytes 2596
  37.7 18.4 %all-to-all-start = ((f32[4,32,8,128]{3,0,2,1:T(4,128)}), f32[4,32,8,128]{3,0,2,1:T(4,128)S(1)}, u32[]{:S(2)}, u32[]{:S(2)}) async-start(f32[4,32,8,128]{3,0,2,1:T(4,128)} %bitcast.8), calls=%async_computation | async-start | bytes 1048576 | tf_op jit(solution)/shard_map/all_to_all | solution.py:62
where the time goes:
time: 67 us; the launch traced here: 66.7 us
  waiting for transfers between devices  20.8 us (31%)
  local copies, waits for them, and re-layouts  15.5 us (23%)
  starting transfers between devices  15.3 us (23%)
  other arithmetic  10.5 us (16%)
  matrix products  3.72 us (6%)
  between operations  0.83 us (1%)
    all_to_all x1, waiting for transfers between devices, shards(): lax.all_to_all(packed, ('gx', 'gy', 'gz'), split_axis=1, concat_axis=1, t...  8.3 us
    all_to_all x1, waiting for transfers between devices, shards(): lax.all_to_all(rim_packed, ('gx', 'gy', 'gz'), split_axis=1, concat_axis=...  5.26 us
    all_to_all x1, starting transfers between devices, shards(): lax.all_to_all(slot_ids, ('gx', 'gy', 'gz'), split_axis=1, concat_axis=1,...  5.1 us
    ppermute x3, starting transfers between devices, from_behind(): return lax.ppermute(block, axis, route)  4.74 us
    all_to_all x1, waiting for transfers between devices, shards(): lax.all_to_all(slot_ids, ('gx', 'gy', 'gz'), split_axis=1, concat_axis=1,...  4.21 us
    unnamed x3, local copies, waits for them, and re-layouts  3.85 us
    dot_general x1, matrix products, shards(): jnp.einsum('oa,alz->olz', table, corners, precision=lax.Precision.HIGHEST)  3.72 us
    sort x1, other arithmetic, shards(): by_owner = jnp.argsort(owner_dev, stable=True)  3.17 us
  transfers between devices with their start and end apart: 6, of which 5 were waited for; matrix products, arithmetic and copies ran while one was open for 27% of the time, Pallas kernels for 0%

commit v1 on v0

v1 whole, which is shorter than its diff:
```python
import functools

import jax
import jax.numpy as jnp
from jax import lax
from jax.experimental import pallas as pl
from jax.experimental.pallas import tpu as pltpu
from jax.sharding import PartitionSpec as P

MESH = pl.DeviceIdType.MESH
AXES = ("gx", "gy", "gz")
F32, BF16, I32 = jnp.float32, jnp.bfloat16, jnp.int32
log_step = 0.3
NN = (((1,), (0,)), ((), ()))
NT = (((1,), (1,)), ((), ()))


def onehot(mask):
    return jnp.where(mask, 1.0, 0.0).astype(BF16)


def split3(x):
    hi = x.astype(BF16)
    rest = x - hi.astype(F32)
    mid = rest.astype(BF16)
    return hi, mid, (rest - mid.astype(F32)).astype(BF16)


def pick(sel, x, dims=NN):
    total = None
    for part in split3(x):
        term = lax.dot_general(sel, part, dims, preferred_element_type=F32)
        total = term if total is None else total + term
    return total


def pick_r(x, sel, dims=NN):
    total = None
    for part in split3(x):
        term = lax.dot_general(part, sel, dims, preferred_element_type=F32)
        total = term if total is None else total + term
    return total


def iota(shape, dim):
    return lax.broadcasted_iota(I32, shape, dim)


def roll_lanes(x, shift):
    width = x.shape[1]
    cut = width - shift % width
    return jnp.concatenate([x[:, cut:], x[:, :cut]], axis=1)


def exchange(
    sizes, cv_ref, ex_ref, own_ref, cur_ref, bef_ref,
    sb1, sb2, rb1, rb2, tx, ty, tc, tr, hx, hy, hc, hr,
    s1_sem, s2_sem, r1_sem, r2_sem, hs_sem, hr_sem,
):
    nx, ny, nz = sizes
    n = nx * ny * nz
    gx, gy, gz = (lax.axis_index(a) for a in AXES)
    me = (gx * ny + gy) * nz + gz
    sx, sy, width = cv_ref.shape
    lines = sx * sy
    s = lines // n

    def coords(d):
        return (d // (ny * nz), (d // nz) % ny, d % nz)

    barrier = pltpu.get_barrier_semaphore()

    def greet(k, carry):
        d = (me + k) % n
        pl.semaphore_signal(barrier, inc=1, device_id=coords(d), device_id_type=MESH)
        return carry

    lax.fori_loop(1, n, greet, 0)

    w3 = cv_ref[...] * jnp.exp(-log_step * ex_ref[...].astype(F32))
    w = w3.reshape(lines, width)
    tx[...] = w[lines - sy :, :]
    ty[...] = w3[:, sy - 1 :, :]
    tc[...] = w[lines - 1 :, :]
    last = onehot(iota((8, width), 1) == width - 1)
    tr[...] = pick(last, w, NT)[0:1, :]

    owner_full = own_ref[...]
    owner = owner_full // lines
    slot = (owner_full % lines).astype(F32)
    mine = owner == iota((n, lines), 0)
    mine_b = onehot(mine)
    below = onehot(iota((lines, lines), 0) < iota((lines, lines), 1))
    counts = lax.dot_general(mine_b, below, NN, preferred_element_type=F32)
    rank = jnp.sum(jnp.where(mine, counts, 0.0), axis=0, keepdims=True).astype(I32)
    place = onehot(owner * s + rank == iota((lines, lines), 0))

    row_id = iota((width, lines), 0)
    at_rank = rank == row_id % s
    group = row_id // s

    packed0 = pick(place, w)
    sb1[:, 0:s, :] = packed0.reshape(n, s, width)
    slots = pick(mine_b, jnp.where(at_rank & (group == 0), slot, 0.0), NT)
    sb1[:, s : s + 1, :] = slots.reshape(n, 1, width)

    pl.semaphore_wait(barrier, n - 1)

    ux, uy, uz = (gx + 1) % nx, (gy + 1) % ny, (gz + 1) % nz
    halo = []
    routes = [
        (tx, hx, (ux, gy, gz)),
        (ty, hy, (gx, uy, gz)),
        (tc, hc, (ux, uy, gz)),
        (tr, hr.at[0], (gx, gy, uz)),
        (tr, hr.at[1], (ux, gy, uz)),
        (tr, hr.at[2], (gx, uy, uz)),
        (tr, hr.at[3], (ux, uy, uz)),
    ]
    for i, (src, dst, to) in enumerate(routes):
        copy = pltpu.make_async_remote_copy(
            src_ref=src, dst_ref=dst, send_sem=hs_sem.at[i], recv_sem=hr_sem.at[i],
            device_id=to, device_id_type=MESH,
        )
        copy.start()
        halo.append(copy)

    def send_all(sb, rb, s_sem, r_sem):
        def send(k, carry):
            d = (me + k) % n
            pltpu.make_async_remote_copy(
                src_ref=sb.at[d], dst_ref=rb.at[me], send_sem=s_sem, recv_sem=r_sem,
                device_id=coords(d), device_id_type=MESH,
            ).start()
            return carry

        lax.fori_loop(n // 2, n, send, 0)
        lax.fori_loop(1, n // 2, send, 0)
        pltpu.make_async_copy(sb.at[me], rb.at[me], r_sem).start()

    send_all(sb1, rb1, s1_sem, r1_sem)

    for copy in halo:
        copy.wait()

    line_id = iota((lines, width), 0)
    first_j = line_id % sy == 0

    def back_j(x, edge):
        edge_full = jnp.broadcast_to(edge, (sx, sy, width)).reshape(lines, width)
        shifted = jnp.concatenate([x[lines - 1 :, :], x[: lines - 1, :]], axis=0)
        return jnp.where(first_j, edge_full, shifted)

    x1 = jnp.concatenate([hx[...], w[: lines - sy, :]], axis=0)
    edge = hy[...]
    x2 = back_j(w, edge)
    x3 = back_j(x1, jnp.concatenate([hc[...].reshape(1, 1, width), edge[: sx - 1]], axis=0))
    for c, x in enumerate((x1, x2, x3)):
        sb2[:, c * s : (c + 1) * s, :] = pick(place, x).reshape(n, s, width)

    lane = iota((1, lines), 1)
    at_j0 = lane % sy == 0
    r0, rx, ry, rxy = hr[0], hr[1], hr[2], hr[3]
    rim1 = jnp.where(lane < sy, roll_lanes(rx, sy), roll_lanes(r0, sy))
    rim2 = jnp.where(at_j0, roll_lanes(ry, 1 - sy), roll_lanes(r0, 1))
    edge_rim = jnp.where(lane == 0, roll_lanes(rxy, 1), roll_lanes(ry, 1))
    rim3 = jnp.where(at_j0, edge_rim, roll_lanes(rim1, 1))
    rims = jnp.where(group == 0, r0, jnp.where(group == 1, rim1, jnp.where(group == 2, rim2, rim3)))
    rims = jnp.where(at_rank & (group < 4), rims, 0.0)
    sb2[:, 3 * s : 3 * s + 1, :] = pick(mine_b, rims, NT).reshape(n, 1, width)

    send_all(sb2, rb2, s2_sem, r2_sem)

    pltpu.make_async_copy(rb1, rb1, r1_sem).wait()
    col_id = iota((width, lines), 1)
    from_dev = iota((n, lines), 1) // s == iota((n, lines), 0)

    def spread(extra, q):
        sel = onehot(row_id == q * s + col_id % s)
        return jnp.sum(jnp.where(from_dev, pick_r(extra, sel), 0.0), axis=0, keepdims=True)

    slot_in = spread(rb1[:, s : s + 1, :].reshape(n, width), 0).astype(I32)
    to_slot = onehot(slot_in == iota((lines, lines), 0))
    cur_ref[0] = pick(to_slot, rb1[:, 0:s, :].reshape(lines, width))

    pltpu.make_async_copy(rb2, rb2, r2_sem).wait()
    for c in range(3):
        cur_ref[c + 1] = pick(to_slot, rb2[:, c * s : (c + 1) * s, :].reshape(lines, width))
    extra = rb2[:, 3 * s : 3 * s + 1, :].reshape(n, width)
    got = [spread(extra, q) for q in range(4)]
    rows = jnp.zeros((width, lines), F32)
    for q in range(4):
        rows = jnp.where(row_id == q, got[q], rows)
    bef_ref[...] = pick(to_slot, rows, NT)

    pltpu.make_async_copy(sb1.at[pl.ds(0, n - 1)], sb1.at[pl.ds(0, n - 1)], s1_sem).wait()
    pltpu.make_async_copy(sb2.at[pl.ds(0, n - 1)], sb2.at[pl.ds(0, n - 1)], s2_sem).wait()


def finish(cur_ref, bef_ref, out_ref, lump_ref):
    shape = cur_ref.shape[1:]
    at_0 = iota(shape, 1) == 0
    near, far = [], []
    for c in range(4):
        x = cur_ref[c] * 0.015625
        shifted = pltpu.roll(x, 1, axis=1)
        near.append(x)
        far.append(jnp.where(at_0, bef_ref[:, c : c + 1] * 0.015625, shifted))

    def triple(c, b):
        return (b, 2.0 * (c + b), c)

    def nine(v):
        by_x0 = triple(v[0], v[1])
        by_x1 = triple(v[2], v[3])
        return [triple(by_x0[o1], by_x1[o1]) for o1 in range(3)]

    cur, back = nine(near), nine(far)
    for o1 in range(3):
        for o2 in range(3):
            for o3, value in enumerate(triple(cur[o1][o2], back[o1][o2])):
                out_ref[9 * o1 + 3 * o2 + o3] = value
    total = functools.reduce(lambda a, b: a + b, near + far)
    lump_ref[...] = 1.0 / (27.0 * total)


def shards(sizes, cell_volume, exponent, owner_row):
    sx, sy, width = cell_volume.shape
    lines = sx * sy
    n = sizes[0] * sizes[1] * sizes[2]
    s = lines // n
    vmem = pl.BlockSpec(memory_space=pltpu.VMEM)
    dma = pltpu.SemaphoreType.DMA
    cur, bef = pl.pallas_call(
        functools.partial(exchange, sizes),
        out_shape=(
            jax.ShapeDtypeStruct((4, lines, width), F32),
            jax.ShapeDtypeStruct((lines, width), F32),
        ),
        in_specs=[vmem] * 3,
        out_specs=(vmem, vmem),
        scratch_shapes=[
            pltpu.VMEM((n, s + 1, width), F32),
            pltpu.VMEM((n, 3 * s + 1, width), F32),
            pltpu.VMEM((n, s + 1, width), F32),
            pltpu.VMEM((n, 3 * s + 1, width), F32),
            pltpu.VMEM((sy, width), F32),
            pltpu.VMEM((sx, 1, width), F32),
            pltpu.VMEM((1, width), F32),
            pltpu.VMEM((1, lines), F32),
            pltpu.VMEM((sy, width), F32),
            pltpu.VMEM((sx, 1, width), F32),
            pltpu.VMEM((1, width), F32),
            pltpu.VMEM((4, 1, lines), F32),
            dma, dma, dma, dma,
            dma((7,)),
            dma((7,)),
        ],
        compiler_params=pltpu.CompilerParams(collective_id=0, has_side_effects=True),
    )(cell_volume, exponent, owner_row.reshape(1, lines))
    rows = 64
    return pl.pallas_call(
        finish,
        grid=(lines // rows,),
        out_shape=(
            jax.ShapeDtypeStruct((27, lines, width), F32),
            jax.ShapeDtypeStruct((lines, width), F32),
        ),
        in_specs=[
            pl.BlockSpec((4, rows, width), lambda i: (0, i, 0)),
            pl.BlockSpec((rows, width), lambda i: (i, 0)),
        ],
        out_specs=(
            pl.BlockSpec((27, rows, width), lambda i: (0, i, 0)),
            pl.BlockSpec((rows, width), lambda i: (i, 0)),
        ),
    )(cur, bef)


def solution(mesh):
    sizes = tuple(mesh.shape[a] for a in AXES)
    return jax.shard_map(
        functools.partial(shards, sizes),
        mesh=mesh,
        in_specs=(P(*AXES), P(*AXES), P(AXES)),
        out_specs=(P(None, AXES, None), P(AXES, None)),
        check_vma=False,
    )
```

time: 67 us -> 28.9 us (0.43)
  Pallas kernels: 0 us -> 28.1 us
  waiting for transfers between devices: 20.8 us -> 0 us
  local copies, waits for them, and re-layouts: 15.5 us -> 0 us
  starting transfers between devices: 15.3 us -> 0 us
  other arithmetic: 10.5 us -> 0 us
  matrix products: 3.72 us -> 0 us
    pallas_call x0 -> x2, Pallas kernels: none -> 28.1 us  [the longest x1 24.1 us: shards(): pl.pallas_call(functools.partial(exchange, sizes), out_shape=(jax.ShapeDt...]
    all_to_all x3 -> x0, waiting for transfers between devices: 17.8 us -> none  [the longest x1 8.3 us: shards(): lax.all_to_all(packed, ('gx', 'gy', 'gz'), split_axis=1, concat_axis=1, t...]
    all_to_all x3 -> x0, starting transfers between devices: 10.6 us -> none  [the longest x1 5.1 us: shards(): lax.all_to_all(slot_ids, ('gx', 'gy', 'gz'), split_axis=1, concat_axis=1,...]
    sort x2 -> x0, other arithmetic: 6.33 us -> none  [the longest x1 3.17 us: shards(): by_owner = jnp.argsort(owner_dev, stable=True)]
    gather x5 -> x0, local copies, waits for them, and re-layouts: 6.15 us -> none  [the longest x1 1.94 us: shards(): slot_ids = (owner_row % line_count)[by_owner].reshape(1, devices_all, -1)]
    ppermute x3 -> x0, starting transfers between devices: 4.74 us -> none  [from_behind(): return lax.ppermute(block, axis, route)]
    unnamed x3 -> x0, local copies, waits for them, and re-layouts: 3.85 us -> none
    dot_general x1 -> x0, matrix products: 3.72 us -> none  [shards(): jnp.einsum('oa,alz->olz', table, corners, precision=lax.Precision.HIGHEST)]
  transfers between devices with their start and end apart: 6 -> 0, of which waited for: 5 -> 0; matrix products, arithmetic and copies ran while one was open for 27% -> 0% of each run, Pallas kernels for 0% -> 0%
where the time goes in v1:
time: 28.9 us; the launch traced here: 28.7 us
  Pallas kernels  28.1 us (97%)
  between operations  0.64 us (2%)
    pallas_call x1, Pallas kernels, shards(): pl.pallas_call(functools.partial(exchange, sizes), out_shape=(jax.ShapeDt...  24.1 us
    pallas_call x1, Pallas kernels, shards(): pl.pallas_call(finish, grid=(lines // rows,), out_shape=(jax.ShapeDtypeSt...  4 us

profile of v1, /device:TPU:0, one launch (start us, length us, event | category | flops | bytes accessed | tf_op | source)
XLA Modules:
  0.0 28.7 jit_solution(17700163277244282933)
XLA Ops:
  0.6 24.1 %shard_map.50 = (f32[4,256,128]{2,1,0:T(8,128)}, f32[256,128]{1,0:T(8,128)}) custom-call(f32[16,16,128]{2,1,0:T(8,128)} %cv_ref.1, s32[16,16,128]{2,1,0:T(8,128)} %ex_ref.1, s32[1,256]{1,0:T(1,128)} %bitcast.1), custom_call_target="tpu_custom_call" | custom-call | tf_op jit(solution)/shard_map/pallas_call | solution.py:234
  24.7 4.0 %shard_map.51 = (f32[27,256,128]{2,1,0:T(8,128)}, f32[256,128]{1,0:T(8,128)}) custom-call(f32[4,256,128]{2,1,0:T(8,128)} %get-tuple-element.4.cur_ref, f32[256,128]{1,0:T(8,128)} %get-tuple-element.5.bef_ref), custom_call_target="tpu_custom_call" | custom-call | tf_op jit(solution)/shard_map/pallas_call | solution.py:262

commit v2 on v1

--- a/solution.py
+++ b/solution.py
@@ -53,9 +53,10 @@
 
 
 def exchange(
-    sizes, cv_ref, ex_ref, own_ref, cur_ref, bef_ref,
-    sb1, sb2, rb1, rb2, tx, ty, tc, tr, hx, hy, hc, hr,
-    s1_sem, s2_sem, r1_sem, r2_sem, hs_sem, hr_sem,
+    sizes, cv_hbm, ex_hbm, own_hbm, cur_ref, bef_ref,
+    cv_ref, ex_ref, own_ref, in_sem,
+    sb1, sb2, sb3, rb1, rb2, rb3, tx, ty, tc, tr, hx, hy, hc, hr,
+    s_sem, r_sem, hs_sem, hr_sem,
 ):
     nx, ny, nz = sizes
     n = nx * ny * nz
@@ -68,6 +69,11 @@
     def coords(d):
         return (d // (ny * nz), (d // nz) % ny, d % nz)
 
+    arrive = []
+    for i, (src, dst) in enumerate(((own_hbm, own_ref), (cv_hbm, cv_ref), (ex_hbm, ex_ref))):
+        copy = pltpu.make_async_copy(src, dst, in_sem.at[i])
+        copy.start()
+        arrive.append(copy)
     barrier = pltpu.get_barrier_semaphore()
 
     def greet(k, carry):
@@ -77,14 +83,7 @@
 
     lax.fori_loop(1, n, greet, 0)
 
-    w3 = cv_ref[...] * jnp.exp(-log_step * ex_ref[...].astype(F32))
-    w = w3.reshape(lines, width)
-    tx[...] = w[lines - sy :, :]
-    ty[...] = w3[:, sy - 1 :, :]
-    tc[...] = w[lines - 1 :, :]
-    last = onehot(iota((8, width), 1) == width - 1)
-    tr[...] = pick(last, w, NT)[0:1, :]
-
+    arrive[0].wait()
     owner_full = own_ref[...]
     owner = owner_full // lines
     slot = (owner_full % lines).astype(F32)
@@ -99,6 +98,16 @@
     at_rank = rank == row_id % s
     group = row_id // s
 
+    arrive[1].wait()
+    arrive[2].wait()
+    w3 = cv_ref[...] * jnp.exp(-log_step * ex_ref[...].astype(F32))
+    w = w3.reshape(lines, width)
+    tx[...] = w[lines - sy :, :]
+    ty[...] = w3[:, sy - 1 :, :]
+    tc[...] = w[lines - 1 :, :]
+    last = onehot(iota((8, width), 1) == width - 1)
+    tr[...] = pick(last, w, NT)[0:1, :]
+
     packed0 = pick(place, w)
     sb1[:, 0:s, :] = packed0.reshape(n, s, width)
     slots = pick(mine_b, jnp.where(at_rank & (group == 0), slot, 0.0), NT)
@@ -109,8 +118,8 @@
     ux, uy, uz = (gx + 1) % nx, (gy + 1) % ny, (gz + 1) % nz
     halo = []
     routes = [
+        (ty, hy, (gx, uy, gz)),
         (tx, hx, (ux, gy, gz)),
-        (ty, hy, (gx, uy, gz)),
         (tc, hc, (ux, uy, gz)),
         (tr, hr.at[0], (gx, gy, uz)),
         (tr, hr.at[1], (ux, gy, uz)),
@@ -125,23 +134,21 @@
         copy.start()
         halo.append(copy)
 
-    def send_all(sb, rb, s_sem, r_sem):
+    def send_all(stage, sb, rb):
         def send(k, carry):
             d = (me + k) % n
             pltpu.make_async_remote_copy(
-                src_ref=sb.at[d], dst_ref=rb.at[me], send_sem=s_sem, recv_sem=r_sem,
+                src_ref=sb.at[d], dst_ref=rb.at[me], send_sem=s_sem.at[stage], recv_sem=r_sem.at[stage],
                 device_id=coords(d), device_id_type=MESH,
             ).start()
             return carry
 
         lax.fori_loop(n // 2, n, send, 0)
-        lax.fori_loop(1, n // 2, send, 0)
-        pltpu.make_async_copy(sb.at[me], rb.at[me], r_sem).start()
-
-    send_all(sb1, rb1, s1_sem, r1_sem)
-
-    for copy in halo:
-        copy.wait()
+        lax.fori_loop(ny * nz, n // 2, send, 0)
+        lax.fori_loop(1, ny * nz, send, 0)
+        pltpu.make_async_copy(sb.at[me], rb.at[me], r_sem.at[stage]).start()
+
+    send_all(0, sb1, rb1)
 
     line_id = iota((lines, width), 0)
     first_j = line_id % sy == 0
@@ -151,12 +158,17 @@
         shifted = jnp.concatenate([x[lines - 1 :, :], x[: lines - 1, :]], axis=0)
         return jnp.where(first_j, edge_full, shifted)
 
+    halo[0].wait()
+    edge = hy[...]
+    sb2[...] = pick(place, back_j(w, edge)).reshape(n, s, width)
+    send_all(1, sb2, rb2)
+
+    for copy in halo[1:]:
+        copy.wait()
     x1 = jnp.concatenate([hx[...], w[: lines - sy, :]], axis=0)
-    edge = hy[...]
-    x2 = back_j(w, edge)
     x3 = back_j(x1, jnp.concatenate([hc[...].reshape(1, 1, width), edge[: sx - 1]], axis=0))
-    for c, x in enumerate((x1, x2, x3)):
-        sb2[:, c * s : (c + 1) * s, :] = pick(place, x).reshape(n, s, width)
+    for c, x in enumerate((x1, x3)):
+        sb3[:, c * s : (c + 1) * s, :] = pick(place, x).reshape(n, s, width)
 
     lane = iota((1, lines), 1)
     at_j0 = lane % sy == 0
@@ -167,11 +179,11 @@
     rim3 = jnp.where(at_j0, edge_rim, roll_lanes(rim1, 1))
     rims = jnp.where(group == 0, r0, jnp.where(group == 1, rim1, jnp.where(group == 2, rim2, rim3)))
     rims = jnp.where(at_rank & (group < 4), rims, 0.0)
-    sb2[:, 3 * s : 3 * s + 1, :] = pick(mine_b, rims, NT).reshape(n, 1, width)
-
-    send_all(sb2, rb2, s2_sem, r2_sem)
-
-    pltpu.make_async_copy(rb1, rb1, r1_sem).wait()
+    sb3[:, 2 * s : 2 * s + 1, :] = pick(mine_b, rims, NT).reshape(n, 1, width)
+
+    send_all(2, sb3, rb3)
+
+    pltpu.make_async_copy(rb1, rb1, r_sem.at[0]).wait()
     col_id = iota((width, lines), 1)
     from_dev = iota((n, lines), 1) // s == iota((n, lines), 0)
 
@@ -183,18 +195,22 @@
     to_slot = onehot(slot_in == iota((lines, lines), 0))
     cur_ref[0] = pick(to_slot, rb1[:, 0:s, :].reshape(lines, width))
 
-    pltpu.make_async_copy(rb2, rb2, r2_sem).wait()
-    for c in range(3):
-        cur_ref[c + 1] = pick(to_slot, rb2[:, c * s : (c + 1) * s, :].reshape(lines, width))
-    extra = rb2[:, 3 * s : 3 * s + 1, :].reshape(n, width)
+    pltpu.make_async_copy(rb2, rb2, r_sem.at[1]).wait()
+    cur_ref[2] = pick(to_slot, rb2[...].reshape(lines, width))
+
+    pltpu.make_async_copy(rb3, rb3, r_sem.at[2]).wait()
+    for c in range(2):
+        cur_ref[2 * c + 1] = pick(to_slot, rb3[:, c * s : (c + 1) * s, :].reshape(lines, width))
+    extra = rb3[:, 2 * s : 2 * s + 1, :].reshape(n, width)
     got = [spread(extra, q) for q in range(4)]
     rows = jnp.zeros((width, lines), F32)
     for q in range(4):
         rows = jnp.where(row_id == q, got[q], rows)
     bef_ref[...] = pick(to_slot, rows, NT)
 
-    pltpu.make_async_copy(sb1.at[pl.ds(0, n - 1)], sb1.at[pl.ds(0, n - 1)], s1_sem).wait()
-    pltpu.make_async_copy(sb2.at[pl.ds(0, n - 1)], sb2.at[pl.ds(0, n - 1)], s2_sem).wait()
+    for stage, sb in enumerate((sb1, sb2, sb3)):
+        sent = sb.at[pl.ds(0, n - 1)]
+        pltpu.make_async_copy(sent, sent, s_sem.at[stage]).wait()
 
 
 def finish(cur_ref, bef_ref, out_ref, lump_ref):
@@ -237,13 +253,16 @@
             jax.ShapeDtypeStruct((4, lines, width), F32),
             jax.ShapeDtypeStruct((lines, width), F32),
         ),
-        in_specs=[vmem] * 3,
+        in_specs=[pl.BlockSpec(memory_space=pltpu.HBM)] * 3,
         out_specs=(vmem, vmem),
         scratch_shapes=[
-            pltpu.VMEM((n, s + 1, width), F32),
-            pltpu.VMEM((n, 3 * s + 1, width), F32),
-            pltpu.VMEM((n, s + 1, width), F32),
-            pltpu.VMEM((n, 3 * s + 1, width), F32),
+            pltpu.VMEM((sx, sy, width), F32),
+            pltpu.VMEM((sx, sy, width), I32),
+            pltpu.VMEM((1, lines), I32),
+            dma((3,)),
+        ]
+        + [pltpu.VMEM((n, rows, width), F32) for rows in (s + 1, s, 2 * s + 1)] * 2
+        + [
             pltpu.VMEM((sy, width), F32),
             pltpu.VMEM((sx, 1, width), F32),
             pltpu.VMEM((1, width), F32),
@@ -252,11 +271,14 @@
             pltpu.VMEM((sx, 1, width), F32),
             pltpu.VMEM((1, width), F32),
             pltpu.VMEM((4, 1, lines), F32),
-            dma, dma, dma, dma,
+            dma((3,)),
+            dma((3,)),
             dma((7,)),
             dma((7,)),
         ],
-        compiler_params=pltpu.CompilerParams(collective_id=0, has_side_effects=True),
+        compiler_params=pltpu.CompilerParams(
+            collective_id=0, has_side_effects=True, vmem_limit_bytes=16 << 20
+        ),
     )(cell_volume, exponent, owner_row.reshape(1, lines))
     rows = 64
     return pl.pallas_call(
@@ -274,6 +296,7 @@
             pl.BlockSpec((27, rows, width), lambda i: (0, i, 0)),
             pl.BlockSpec((rows, width), lambda i: (i, 0)),
         ),
+        compiler_params=pltpu.CompilerParams(vmem_limit_bytes=16 << 20),
     )(cur, bef)
 
 

time: 28.9 us -> 28.2 us (0.976)
  Pallas kernels: 28.1 us -> 24.9 us
  local copies, waits for them, and re-layouts: 0 us -> 2.48 us
    unnamed x0 -> x6, local copies, waits for them, and re-layouts: none -> 2.48 us
    pallas_call x1, Pallas kernels: 24.1 us -> 22.3 us  [shards(): pl.pallas_call(functools.partial(exchange, sizes), out_shape=(jax.ShapeDt...]
    pallas_call x1, Pallas kernels: 4 us -> 2.53 us  [shards(): pl.pallas_call(finish, grid=(lines // rows,), out_shape=(jax.ShapeDtypeSt...]
where the time goes in v2:
time: 28.2 us; the launch traced here: 28 us
  Pallas kernels  24.9 us (88%)
  local copies, waits for them, and re-layouts  2.48 us (9%)
  between operations  0.65 us (2%)
    pallas_call x1, Pallas kernels, shards(): pl.pallas_call(functools.partial(exchange, sizes), out_shape=(jax.ShapeDt...  22.3 us
    pallas_call x1, Pallas kernels, shards(): pl.pallas_call(finish, grid=(lines // rows,), out_shape=(jax.ShapeDtypeSt...  2.53 us
    unnamed x6, local copies, waits for them, and re-layouts  2.48 us

profile of v2, /device:TPU:0, one launch (start us, length us, event | category | flops | bytes accessed | tf_op | source)
XLA Modules:
  0.0 28.0 jit_solution(17683564577716725918)
XLA Ops:
  0.6 0.0 copy-start
  0.6 0.9 %copy-done = f32[16,16,128]{2,1,0:T(8,128)S(1)} copy-done((f32[16,16,128]{2,1,0:T(8,128)S(1)}, f32[16,16,128]{2,1,0:T(8,128)}, u32[]{:S(2)}) %copy-start) | copy-done | bytes 131096
  1.5 0.0 copy-start.1
  1.5 0.9 %copy-done.1 = s32[16,16,128]{2,1,0:T(8,128)S(1)} copy-done((s32[16,16,128]{2,1,0:T(8,128)S(1)}, s32[16,16,128]{2,1,0:T(8,128)}, u32[]{:S(2)}) %copy-start.1) | copy-done | bytes 131096
  2.4 0.0 copy-start.2
  2.4 0.7 %copy-done.2 = s32[256]{0:T(256)S(1)} copy-done((s32[256]{0:T(256)S(1)}, s32[256]{0:T(256)}, u32[]{:S(2)}) %copy-start.2) | copy-done | bytes 1048
  3.1 22.3 %shard_map.50 = (f32[4,256,128]{2,1,0:T(8,128)S(1)}, f32[256,128]{1,0:T(8,128)S(1)}) custom-call(f32[16,16,128]{2,1,0:T(8,128)S(1)} %copy-done, s32[16,16,128]{2,1,0:T(8,128)S(1)} %copy-done.1, s32[1,256]{1,0:T(1,128)S(1)} %bitcast.1), custom_call_target="tpu_custom_call" | custom-call | tf_op jit(solution)/shard_map/pallas_call | solution.py:250
  25.5 2.5 %shard_map.51 = (f32[27,256,128]{2,1,0:T(8,128)}, f32[256,128]{1,0:T(8,128)}) custom-call(f32[4,256,128]{2,1,0:T(8,128)S(1)} %get-tuple-element.4.cur_ref, f32[256,128]{1,0:T(8,128)S(1)} %get-tuple-element.5.bef_ref), custom_call_target="tpu_custom_call" | custom-call | tf_op jit(solution)/shard_map/pallas_call | solution.py:284
Async XLA Ops:
  0.6 0.9 %copy-start = (f32[16,16,128]{2,1,0:T(8,128)S(1)}, f32[16,16,128]{2,1,0:T(8,128)}, u32[]{:S(2)}) copy-start(f32[16,16,128]{2,1,0:T(8,128)} %cv_hbm.1) | copy-start | bytes 393220
  1.5 0.9 %copy-start.1 = (s32[16,16,128]{2,1,0:T(8,128)S(1)}, s32[16,16,128]{2,1,0:T(8,128)}, u32[]{:S(2)}) copy-start(s32[16,16,128]{2,1,0:T(8,128)} %ex_hbm.1) | copy-start | bytes 393220
  2.4 0.7 %copy-start.2 = (s32[256]{0:T(256)S(1)}, s32[256]{0:T(256)}, u32[]{:S(2)}) copy-start(s32[256]{0:T(256)} %param.5) | copy-start | bytes 3076

commit v3 on v2

--- a/solution.py
+++ b/solution.py
@@ -19,16 +19,14 @@
     return jnp.where(mask, 1.0, 0.0).astype(BF16)
 
 
-def split3(x):
+def halves(x):
     hi = x.astype(BF16)
-    rest = x - hi.astype(F32)
-    mid = rest.astype(BF16)
-    return hi, mid, (rest - mid.astype(F32)).astype(BF16)
+    return hi, (x - hi.astype(F32)).astype(BF16)
 
 
 def pick(sel, x, dims=NN):
     total = None
-    for part in split3(x):
+    for part in halves(x):
         term = lax.dot_general(sel, part, dims, preferred_element_type=F32)
         total = term if total is None else total + term
     return total
@@ -36,7 +34,7 @@
 
 def pick_r(x, sel, dims=NN):
     total = None
-    for part in split3(x):
+    for part in halves(x):
         term = lax.dot_general(part, sel, dims, preferred_element_type=F32)
         total = term if total is None else total + term
     return total
@@ -136,7 +134,9 @@
 
     def send_all(stage, sb, rb):
         def send(k, carry):
-            d = (me + k) % n
+            a, r = k // (ny * nz), k % (ny * nz)
+            px, py, pz = (gx + a) % nx, (gy + r // nz) % ny, (gz + r % nz) % nz
+            d = (px * ny + py) * nz + pz
             pltpu.make_async_remote_copy(
                 src_ref=sb.at[d], dst_ref=rb.at[me], send_sem=s_sem.at[stage], recv_sem=r_sem.at[stage],
                 device_id=coords(d), device_id_type=MESH,
@@ -279,8 +279,8 @@
         compiler_params=pltpu.CompilerParams(
             collective_id=0, has_side_effects=True, vmem_limit_bytes=16 << 20
         ),
-    )(cell_volume, exponent, owner_row.reshape(1, lines))
-    rows = 64
+    )(*(pltpu.with_memory_space_constraint(a, pltpu.HBM) for a in (cell_volume, exponent, owner_row.reshape(1, lines))))
+    rows = 128
     return pl.pallas_call(
         finish,
         grid=(lines // rows,),

time: 28.2 us -> 23.5 us (0.83)
  local copies, waits for them, and re-layouts: 2.48 us -> 0 us
  Pallas kernels: 24.9 us -> 22.7 us
    unnamed x6 -> x0, local copies, waits for them, and re-layouts: 2.48 us -> none
    pallas_call x1, Pallas kernels: 22.3 us -> 20.6 us  [shards(): pl.pallas_call(functools.partial(exchange, sizes), out_shape=(jax.ShapeDt...]
    pallas_call x1, Pallas kernels: 2.53 us -> 2.14 us  [shards(): pl.pallas_call(finish, grid=(lines // rows,), out_shape=(jax.ShapeDtypeSt...]
where the time goes in v3:
time: 23.5 us; the launch traced here: 23.4 us
  Pallas kernels  22.7 us (97%)
  between operations  0.64 us (3%)
    pallas_call x1, Pallas kernels, shards(): pl.pallas_call(functools.partial(exchange, sizes), out_shape=(jax.ShapeDt...  20.6 us
    pallas_call x1, Pallas kernels, shards(): pl.pallas_call(finish, grid=(lines // rows,), out_shape=(jax.ShapeDtypeSt...  2.14 us

profile of v3, /device:TPU:0, one launch (start us, length us, event | category | flops | bytes accessed | tf_op | source)
XLA Modules:
  0.0 23.4 jit_solution(7770030529289971404)
XLA Ops:
  0.6 20.6 %shard_map.50 = (f32[4,256,128]{2,1,0:T(8,128)S(1)}, f32[256,128]{1,0:T(8,128)S(1)}) custom-call(f32[16,16,128]{2,1,0:T(8,128)} %cv_hbm.1, s32[16,16,128]{2,1,0:T(8,128)} %ex_hbm.1, s32[1,256]{1,0:T(1,128)} %bitcast.1), custom_call_target="tpu_custom_call" | custom-call | tf_op jit(solution)/shard_map/pallas_call | solution.py:250
  21.2 2.1 %shard_map.51 = (f32[27,256,128]{2,1,0:T(8,128)}, f32[256,128]{1,0:T(8,128)}) custom-call(f32[4,256,128]{2,1,0:T(8,128)S(1)} %get-tuple-element.4.cur_ref, f32[256,128]{1,0:T(8,128)S(1)} %get-tuple-element.5.bef_ref), custom_call_target="tpu_custom_call" | custom-call | tf_op jit(solution)/shard_map/pallas_call | solution.py:284
